TPU v7x, 32 devices: a whole 2x2x4 slice. The times are simulated.
32 devices in a mesh: slab: 16 (over z, y, x), sub: 2 (over core).
Axes of the slice: x: 2, y: 2, z: 4, core: 2. Of those that a mesh axis runs over, the one named last changes fastest.
Arguments:
- start: float32 [4, 96, 32, 256], P(None, 'slab', 'sub'), may hold values from -6 to 6
- wind: float32 [3, 96, 32, 256], P(None, 'slab', 'sub'), may hold values from -4 to 4
- reaction: float32 [96, 32, 256], P('slab', 'sub'), may hold values from 0.5 to 4
- mass: float32 [96, 32, 256], P('slab', 'sub'), may hold values from 0.5 to 2
Outputs:
- basis: float32 [4, 4, 96, 32, 256], P(None, None, 'slab', 'sub')
- search: float32 [3, 4, 96, 32, 256], P(None, None, 'slab', 'sub')
- hessenberg: float32 [4, 3], replicated
All inputs are finite; a program needn't handle non-finite values.
Results may differ from a plain program's by a relative error of at most 0.0003.
Values sent between devices are 32-bit elements; how exact they have to be, the bound alone decides.
A program may use at most 64 MiB of HBM per device.

v0:
```python
import functools

import jax
import jax.numpy as jnp
from jax import lax
from jax.experimental import pallas as pl
from jax.experimental.pallas import tpu as pltpu
from jax.sharding import PartitionSpec as P

ITERS = 3
UNROLL = 5
WP, WU, WC, WQ = 2, 2, 2, 3
HALO = 8
LANES = 128
MESH = pl.DeviceIdType.MESH


def fold(x):
    rows, cols = x.shape
    total = None
    for r in range(0, rows, 8):
        for c in range(0, cols, LANES):
            piece = x[r : r + 8, c : c + LANES]
            total = piece if total is None else total + piece
    return total


def kernel(
    slabs, subs, cx, cy, nz,
    start, wind, reaction, mass, basis, search, hess,
    xp, xu, vp, vu, raw, co, mk, t1, qs, y0, y1, wl, ob, os_, red,
    send, recv, red_send, red_recv, load, store,
):
    slab, sub = lax.axis_index("slab"), lax.axis_index("sub")
    n = slabs * subs
    me = slab * subs + sub
    rows = cy + HALO
    has_left, has_right = slab > 0, slab < slabs - 1

    loads = [
        pltpu.make_async_copy(start.at[3], xp.at[0, pl.ds(WP, cx), pl.ds(0, cy)], load.at[0]),
        pltpu.make_async_copy(
            start.at[pl.ds(0, 3)], xu.at[0, :, pl.ds(WU, cx), pl.ds(0, cy)], load.at[1]
        ),
        pltpu.make_async_copy(
            wind, raw.at[pl.ds(0, 3), pl.ds(WC, cx), pl.ds(0, cy)], load.at[2]
        ),
        pltpu.make_async_copy(reaction, raw.at[3, pl.ds(WC, cx), pl.ds(0, cy)], load.at[3]),
        pltpu.make_async_copy(mass, raw.at[4, pl.ds(WC, cx), pl.ds(0, cy)], load.at[4]),
    ]
    for item in loads:
        item.start()

    barrier = pltpu.get_barrier_semaphore()

    def greet(k, carry):
        for other in range(subs):
            pl.semaphore_signal(
                barrier, inc=1, device_id=(lax.rem(slab + k, slabs), other), device_id_type=MESH
            )
        return carry

    for k in range(1, subs):
        pl.semaphore_signal(
            barrier, inc=1, device_id=(slab, lax.rem(sub + k, subs)), device_id_type=MESH
        )
    lax.fori_loop(1, slabs, greet, 0)

    def clear(low):
        def inner():
            for e in range(ITERS):
                for k in range(WP):
                    at = k if low else WP + cx + k
                    xp[e, at, 0:cy] = jnp.zeros((cy, nz), jnp.float32)
                for k in range(WQ):
                    at = k if low else WQ + cx + k
                    qs[e, at, 0:cy] = jnp.zeros((cy, nz), jnp.float32)
                for c in range(3):
                    for k in range(WU):
                        at = k if low else WU + cx + k
                        xu[e, c, at, 0:cy] = jnp.zeros((cy, nz), jnp.float32)
            for c in range(5):
                for k in range(WC):
                    at = k if low else WC + cx + k
                    raw[c, at, 0:cy] = jnp.zeros((cy, nz), jnp.float32)
        return inner

    pl.when(jnp.logical_not(has_left))(clear(True))
    pl.when(jnp.logical_not(has_right))(clear(False))

    row = lax.broadcasted_iota(jnp.int32, (rows, nz), 0)
    col = lax.broadcasted_iota(jnp.int32, (rows, nz), 1)
    last = jnp.where(sub == 0, rows - 1, cy - 1)
    first = jnp.where(sub == 0, 0, cy)
    mk[0] = jnp.where(row == last, 0.0, 1.0)
    mk[1] = jnp.where(row == first, 0.0, 1.0)
    mk[2] = jnp.where(col == nz - 1, 0.0, 1.0)
    mk[3] = jnp.where(col == 0, 0.0, 1.0)

    pl.semaphore_wait(barrier, n - 1)

    def p_view(e):
        return lambda planes, lines: xp.at[e, planes, lines]

    def u_view(e):
        return lambda planes, lines: xu.at[e, :, planes, lines]

    def q_view(e):
        return lambda planes, lines: qs.at[e, planes, lines]

    def wind_view(planes, lines):
        return raw.at[pl.ds(0, 3), planes, lines]

    def row_view(i):
        return lambda planes, lines: raw.at[i, planes, lines]

    every, across = (0, 1, 2, 3, 4), (0, 1, 3, 4)
    groups = [
        (p_view(0), WP, WP, every), (u_view(0), WU, WU, every),
        (row_view(3), WC, WC, every),
        (p_view(1), WP, WP, every), (u_view(1), WU, WU, every),
        (p_view(2), WP, WP, every), (u_view(2), WU, WU, every),
        (wind_view, WC, 1, every), (row_view(4), WC, 0, (2,)),
        (q_view(0), WQ, WQ, across), (q_view(1), WQ, WQ, across), (q_view(2), WQ, WQ, across),
    ]
    own_lines = pl.ds(0, cy)
    edge_lines = pl.ds(pl.multiple_of((1 - sub) * (cy - HALO), 8), HALO)
    halo_lines = pl.ds(cy, HALO)

    def remote(g, kind):
        view, base, w, _ = groups[g]
        end = base + cx
        if kind == 0:
            src, dst = view(pl.ds(end - w, w), own_lines), view(pl.ds(base - w, w), own_lines)
            target = {"slab": slab + 1}
        elif kind == 1:
            src, dst = view(pl.ds(base, w), own_lines), view(pl.ds(end, w), own_lines)
            target = {"slab": slab - 1}
        else:
            planes = (pl.ds(base, cx), pl.ds(base - w, w), pl.ds(end, w))[kind - 2]
            src, dst = view(planes, edge_lines), view(planes, halo_lines)
            target = {"sub": 1 - sub}
        return pltpu.make_async_remote_copy(
            src_ref=src, dst_ref=dst, send_sem=send.at[g, kind], recv_sem=recv.at[g, kind],
            device_id=target, device_id_type=MESH,
        )

    def begin(g, chosen=(0, 1, 2)):
        kinds = [kind for kind in groups[g][3] if kind in chosen]
        if 0 in kinds:
            pl.when(has_right)(lambda: remote(g, 0).start())
            pl.when(has_left)(lambda: remote(g, 1).start())
        if 2 in kinds:
            remote(g, 2).start()

    def forward(g):
        if 0 in groups[g][3]:
            pl.when(has_left)(lambda: remote(g, 0).wait_recv())
            remote(g, 3).start()
            pl.when(has_right)(lambda: remote(g, 1).wait_recv())
            remote(g, 4).start()

    def arrive(g, kinds=(2, 3, 4)):
        for kind in groups[g][3]:
            if kind in kinds:
                remote(g, kind).wait_recv()

    def finish(g):
        for kind in groups[g][3]:
            if kind == 0:
                pl.when(has_right)(lambda: remote(g, 0).wait_send())
            elif kind == 1:
                pl.when(has_left)(lambda: remote(g, 1).wait_send())
            else:
                remote(g, kind).wait_send()

    lane = lax.broadcasted_iota(jnp.int32, (1, LANES), 1)

    def reduce_start(e, parts):
        line = jnp.zeros((1, LANES), jnp.float32)
        for i, part in enumerate(parts):
            line = line + jnp.where(lane == i, jnp.sum(fold(part), keepdims=True), 0.0)
        red[e, me] = line

        def tell(at, core):
            pltpu.make_async_remote_copy(
                src_ref=red.at[e, me], dst_ref=red.at[e, me],
                send_sem=red_send.at[e], recv_sem=red_recv.at[e],
                device_id=(at, core), device_id_type=MESH,
            ).start()

        def push(k, carry):
            at = lax.rem(slab + k, slabs)
            for core in range(subs):
                tell(at, core)
            return carry

        lax.fori_loop(1, slabs, push, 0)
        for k in range(1, subs):
            tell(slab, lax.rem(sub + k, subs))

    def red_wait(e, sem):
        block = red.at[e, pl.ds(0, n - 1)]
        pltpu.make_async_copy(block, block, sem.at[e]).wait()

    def reduce_end(e, count):
        red_wait(e, red_recv)
        total = jnp.sum(red[e], axis=0)
        return [
            jnp.sum(jnp.where(lane == i, total, 0.0), axis=1, keepdims=True)
            for i in range(count)
        ]

    def turn(f):
        return (
            pltpu.roll(f, rows - 1, 0), pltpu.roll(f, 1, 0),
            pltpu.roll(f, nz - 1, 1), pltpu.roll(f, 1, 1),
        )

    def masked(f):
        yp, ym, zp, zm = turn(f)
        return yp * mk[0], ym * mk[1], zp * mk[2], zm * mk[3]

    def off_diagonal(below, around, above, k):
        yp, ym, zp, zm = around
        total = co[0, k] * above + co[1, k] * below
        total = total + (co[2, k] * yp + co[3, k] * ym)
        return total + (co[4, k] * zp + co[5, k] * zm)

    def loop(count, body, init=0, low=0):
        step = max(u for u in range(1, UNROLL + 1) if count % u == 0)

        def several(k, carry):
            for i in range(step):
                carry = body(low + k * step + i, carry)
            return carry

        return lax.fori_loop(0, count // step, several, init)

    def spans(spans_of, body):
        for low, high in spans_of:
            if high > low:
                loop(high - low, body, low=low)

    def inside(k, w):
        at = slab * cx + k - w
        return jnp.logical_and(at >= 0, at < slabs * cx)

    def coefficients(where):
        def body(k, carry):
            ok = jnp.where(inside(k, WC), 1.0, 0.0)
            keep = jnp.full((rows, nz), ok) > 0.5
            hx, hy, hz = 0.5 * raw[0, k], 0.5 * raw[1, k], 0.5 * raw[2, k]
            co[0, k] = 1.0 - hx
            co[1, k] = 1.0 + hx
            co[2, k] = (1.0 - hy) * mk[0]
            co[3, k] = (1.0 + hy) * mk[1]
            co[4, k] = (1.0 - hz) * mk[2]
            co[5, k] = (1.0 + hz) * mk[3]
            diagonal = 6.0 + raw[3, k]
            co[6, k] = diagonal
            co[7, k] = jnp.where(keep, 1.0 / diagonal, 0.0)
            co[8, k] = jnp.where(keep, 1.0 / raw[4, k], 0.0)
            return carry

        spans(where, body)

    def first_guess(p):
        def body(k, carry):
            here = p[k + 1]
            yp, ym, zp, zm = masked(here)
            total = (p[k] + p[k + 2]) + (yp + ym) + (zp + zm)
            ok = jnp.where(inside(k, WP - 1), 1.0 / 7.0, 0.0)
            t1[k] = (here + total * (1.0 / 7.0)) * ok
            return carry

        loop(cx + 2 * (WP - 1), body)

    def schur(qq):
        def body(k, carry):
            here = t1[k + 1]
            off = off_diagonal(t1[k], turn(here), t1[k + 2], k + WC)
            qq[k + WQ] = (off - co[6, k + WC] * here) * co[8, k + WC]
            return carry

        loop(cx, body)

    def velocity_first(qq, u, where):
        def body(k, carry):
            yp, ym, zp, zm = masked(qq[k + 1])
            scale = co[7, k]
            y0[0, k] = (u[0, k] - 0.5 * (qq[k + 2] - qq[k])) * scale
            y0[1, k] = (u[1, k] - 0.5 * (yp - ym)) * scale
            y0[2, k] = (u[2, k] - 0.5 * (zp - zm)) * scale
            return carry

        spans(where, body)

    def velocity_second(where):
        def body(k, carry):
            scale = co[7, k + 1]
            for c in range(3):
                here = y0[c, k + 1]
                off = off_diagonal(y0[c, k], turn(here), y0[c, k + 2], k + 1)
                y1[c, k] = here + off * scale
            return carry

        spans(where, body)

    def image(e, qq, vectors):
        def body(k, acc):
            q = qq[k + WQ]
            qa, qb = qq[k + WQ + 1], qq[k + WQ - 1]
            yp, ym, zp, zm = masked(q)
            grads = (0.5 * (qa - qb), 0.5 * (yp - ym), 0.5 * (zp - zm))
            low = 0.5 * ((qa + qb) + (yp + ym) + (zp + zm)) - 3.0 * q
            out = []
            for c in range(3):
                here = y1[c, k + 1]
                below, above = y1[c, k], y1[c, k + 2]
                around = turn(here)
                off = off_diagonal(below, around, above, k + WC)
                w = (co[6, k + WC] * here - off + grads[c])[:cy]
                if c == 0:
                    low = low - 0.5 * (above - below)
                elif c == 1:
                    low = low - 0.5 * (around[0] * mk[0] - around[1] * mk[1])
                else:
                    low = low - 0.5 * (around[2] * mk[2] - around[3] * mk[3])
                os_[e, c, k] = here[:cy]
                out.append(w)
            os_[e, 3, k] = q[:cy]
            out.append(low[:cy])
            if e + 1 < ITERS:
                for c in range(3):
                    xu[e + 1, c, k + WU, 0:cy] = out[c]
                xp[e + 1, k + WP, 0:cy] = out[3]
            else:
                for c in range(4):
                    wl[c, k] = out[c]
            acc = list(acc)
            for i, (p, u) in enumerate(vectors):
                held = [u[c, k + WU, 0:cy] for c in range(3)] + [p[k + WP, 0:cy]]
                term = held[0] * out[0] + held[1] * out[1]
                acc[i + 1] = acc[i + 1] + (term + (held[2] * out[2] + held[3] * out[3]))
                if i == e:
                    term = held[0] * held[0] + held[1] * held[1]
                    acc[0] = acc[0] + (term + (held[2] * held[2] + held[3] * held[3]))
            return tuple(acc)

        zero = jnp.zeros((cy, nz), jnp.float32)
        acc = (zero,) * (e + 2)
        acc = loop(WP, body, acc)
        acc = loop(WP, body, acc, low=cx - WP)
        if e + 1 < ITERS:
            begin((3, 5)[e], (0, 1))
        acc = loop(cx - 2 * WP, body, acc, low=WP)
        if e + 1 < ITERS:
            begin((3, 5)[e], (2,))
        return acc

    def write_out(e):
        return (
            pltpu.make_async_copy(ob.at[e], basis.at[e], store.at[0, e]),
            pltpu.make_async_copy(os_.at[e], search.at[e], store.at[1, e]),
        )

    def results(e, vector, inverse):
        p, u = vector

        def body(k, carry):
            for c in range(3):
                ob[e, c, k] = u[c, k + WU, 0:cy] * inverse
            ob[e, 3, k] = p[k + WP, 0:cy] * inverse
            for c in range(4):
                os_[e, c, k] = os_[e, c, k] * inverse
            return carry

        loop(cx, body)
        for item in write_out(e):
            item.start()

    loads[0].wait()
    begin(0)
    for item in loads[2:]:
        item.wait()
    for g in (2, 7, 8):
        begin(g, (2,))
    loads[1].wait()
    begin(1)
    for g in (2, 7):
        begin(g, (0, 1))
    for g in (2, 7, 8):
        arrive(g, (2,))
    coefficients([(WC, WC + cx)])
    forward(0)
    arrive(0)

    vectors = [(xp.at[0], xu.at[0])]
    inverses = []
    entries = {}
    first_guess(vectors[0][0])
    for e in range(ITERS):
        p, u = vectors[e]
        p_group, u_group = ((0, 1), (3, 4), (5, 6))[e]
        if e > 0:
            first_guess(p)
        qq = qs.at[e]
        schur(qq)
        begin(9 + e)
        if e > 0:
            results(e - 1, vectors[e - 1], inverses[e - 1])
        end_u, end_1 = cx + 2 * WU, cx + 2
        deep = min(3, end_1 // 2)
        inner = (WU + 1, WU + cx - 1)
        arrive(u_group, (2,))
        if e > 0:

            def form_u(k, carry, e=e):
                for c in range(3):
                    total = xu[e, c, k] * factor
                    for g, (_, other) in zip(weights, vectors[:e]):
                        total = total - g * other[c, k]
                    u[c, k] = total
                return carry

            spans([(WU, WU + cx)], form_u)
        velocity_first(qq, u, [inner])
        velocity_second([(deep, end_1 - deep)])
        forward(u_group)
        if e == 0:
            for g in (2, 7):
                forward(g)
            for g in (2, 7):
                arrive(g, (3, 4))
            coefficients([(0, WC), (WC + cx, cx + 2 * WC)])
        forward(9 + e)
        arrive(u_group, (3, 4))
        if e > 0:
            spans([(0, WU), (WU + cx, end_u)], form_u)
        arrive(9 + e)
        velocity_first(qq, u, [(0, inner[0]), (inner[1], end_u)])
        velocity_second([(0, deep), (end_1 - deep, end_1)])
        acc = image(e, qq, vectors)
        reduce_start(e, acc)
        if e + 1 < ITERS:
            begin(u_group + 3 if e == 0 else 6)
        sums = reduce_end(e, e + 2)
        norm = jnp.sqrt(sums[0])
        factor = 1.0 / norm
        if e > 0:
            entries[(e, e - 1)] = norm
        inverses.append(factor)
        weights = []
        for i in range(e + 1):
            h = sums[i + 1] * inverses[i] * factor
            entries[(i, e)] = h
            weights.append(h * inverses[i])
        if e + 1 < ITERS:
            g_p = (3, 5)[e]
            forward(g_p)
            arrive(g_p)
            new = (vp.at[e], vu.at[e])

            def form_p(k, carry, e=e):
                total = xp[e + 1, k] * factor
                for g, (other, _) in zip(weights, vectors[: e + 1]):
                    total = total - g * other[k]
                vp[e, k] = total
                return carry

            loop(cx + 2 * WP, form_p)
            vectors.append(new)

    def close(k, acc):
        for c in range(4):
            total = wl[c, k] * factor
            for g, (p, u) in zip(weights, vectors):
                held = p[k + WP, 0:cy] if c == 3 else u[c, k + WU, 0:cy]
                total = total - g * held
            ob[ITERS, c, k] = total
            acc = acc + total * total
        return acc

    acc = loop(cx, close, jnp.zeros((cy, nz), jnp.float32))
    reduce_start(ITERS, [acc])
    results(ITERS - 1, vectors[ITERS - 1], inverses[ITERS - 1])
    for g in range(len(groups)):
        finish(g)
    norm = jnp.sqrt(reduce_end(ITERS, 1)[0])
    entries[(ITERS, ITERS - 1)] = norm
    factor = 1.0 / norm

    def scale(k, carry):
        for c in range(4):
            ob[ITERS, c, k] = ob[ITERS, c, k] * factor
        return carry

    loop(cx, scale)
    final = pltpu.make_async_copy(ob.at[ITERS], basis.at[ITERS], store.at[0, ITERS])
    final.start()
    r = lax.broadcasted_iota(jnp.int32, (ITERS + 1, ITERS), 0)
    c = lax.broadcasted_iota(jnp.int32, (ITERS + 1, ITERS), 1)
    table = jnp.zeros((ITERS + 1, ITERS), jnp.float32)
    for (i, j), value in entries.items():
        table = table + jnp.where(jnp.logical_and(r == i, c == j), value, 0.0)
    hess[...] = table
    for e in range(ITERS + 1):
        red_wait(e, red_send)
    for e in range(ITERS):
        for item in write_out(e):
            item.wait()
    final.wait()


def per_device(slabs, subs, start, wind, reaction, mass):
    _, cx, cy, nz = start.shape
    n = slabs * subs
    rows = cy + HALO
    f32 = jnp.float32

    def field(*lead):
        return pltpu.VMEM((*lead, rows, nz), f32)

    out_shape = (
        jax.ShapeDtypeStruct((ITERS + 1, 4, cx, cy, nz), f32),
        jax.ShapeDtypeStruct((ITERS, 4, cx, cy, nz), f32),
        jax.ShapeDtypeStruct((ITERS + 1, ITERS), f32),
    )
    anywhere = pl.BlockSpec(memory_space=pl.ANY)
    return pl.pallas_call(
        functools.partial(kernel, slabs, subs, cx, cy, nz),
        out_shape=out_shape,
        in_specs=[pl.BlockSpec(memory_space=pltpu.HBM)] * 4,
        out_specs=(anywhere, anywhere, pl.BlockSpec(memory_space=pltpu.VMEM)),
        scratch_shapes=[
            field(ITERS, cx + 2 * WP),
            field(ITERS, 3, cx + 2 * WU),
            field(ITERS - 1, cx + 2 * WP),
            field(ITERS - 1, 3, cx + 2 * WU),
            field(5, cx + 2 * WC),
            field(9, cx + 2 * WC),
            field(4),
            field(cx + 2 * (WP - 1)),
            field(ITERS, cx + 2 * WQ),
            field(3, cx + 2 * WU),
            field(3, cx + 2),
            pltpu.VMEM((4, cx, cy, nz), f32),
            pltpu.VMEM((ITERS + 1, 4, cx, cy, nz), f32),
            pltpu.VMEM((ITERS, 4, cx, cy, nz), f32),
            pltpu.VMEM((ITERS + 1, n, 1, LANES), f32),
            pltpu.SemaphoreType.DMA((12, 5)),
            pltpu.SemaphoreType.DMA((12, 5)),
            pltpu.SemaphoreType.DMA((ITERS + 1,)),
            pltpu.SemaphoreType.DMA((ITERS + 1,)),
            pltpu.SemaphoreType.DMA((5,)),
            pltpu.SemaphoreType.DMA((2, ITERS + 1)),
        ],
        compiler_params=pltpu.CompilerParams(
            collective_id=0, has_side_effects=True, vmem_limit_bytes=63_900_000
        ),
    )(start, wind, reaction, mass)


def solution(mesh):
    slabs, subs = mesh.shape["slab"], mesh.shape["sub"]
    return jax.shard_map(
        functools.partial(per_device, slabs, subs),
        mesh=mesh,
        in_specs=(
            P(None, "slab", "sub", None),
            P(None, "slab", "sub", None),
            P("slab", "sub", None),
            P("slab", "sub", None),
        ),
        out_specs=(P(None, None, "slab", "sub", None), P(None, None, "slab", "sub", None), P()),
        check_vma=False,
    )
```

profile of v0, /device:TPU:0, one launch (start us, length us, event | category | flops | bytes accessed | tf_op | source)
XLA Modules:
  0.0 66.4 jit_solution(2283616478409074870)
XLA Ops:
  0.6 61.3 %shard_map.67 = (f32[4,4,6,16,256]{4,3,2,1,0:T(8,128)}, f32[3,4,6,16,256]{4,3,2,1,0:T(8,128)}, f32[4,3]{1,0:T(4,128)}) custom-call(f32[4,6,16,256]{3,2,1,0:T(8,128)} %start.1, f32[3,6,16,256]{3,2,1,0:T(8,128)} %wind.1, f32[6,16,256]{2,1,0:T(8,128)} %reaction.1, f32[6,16,256]{2,1,0:T(8,128)} %mass.1), custom_call_target="tpu_custom_call" | custom-call | tf_op jit(solution)/shard_map/pallas_call | solution.py:531
  61.9 0.0 copy-start
  62.0 2.8 %copy.10 = f32[4,4,6,16,256]{4,3,2,1,0:T(8,128)} copy(f32[4,4,6,16,256]{4,3,2,1,0:T(8,128)} %get-tuple-element.6) | data formatting | bytes 3145728
  64.8 0.0 copy-done
  64.8 0.0 copy-start.1
  64.8 1.0 %copy.11 = f32[3,4,6,16,256]{4,3,2,1,0:T(8,128)} copy(f32[3,4,6,16,256]{4,3,2,1,0:T(8,128)S(1)} %copy-done) | data formatting | bytes 2359296
  65.8 0.0 copy-done.1
  65.8 0.6 copy.12
Async XLA Ops:
  61.9 2.8 %copy-start = (f32[3,4,6,16,256]{4,3,2,1,0:T(8,128)S(1)}, f32[3,4,6,16,256]{4,3,2,1,0:T(8,128)}, u32[]{:S(2)}) copy-start(f32[3,4,6,16,256]{4,3,2,1,0:T(8,128)} %get-tuple-element.7) | copy-start | bytes 3538948
  64.8 1.0 %copy-start.1 = (f32[4,3]{1,0:T(4,128)S(1)}, f32[4,3]{1,0:T(4,128)}, u32[]{:S(2)}) copy-start(f32[4,3]{1,0:T(4,128)} %get-tuple-element.8) | copy-start | bytes 148
where the time goes:
time: 66.5 us; the launch traced here: 66.4 us
  Pallas kernels  61.3 us (92%)
  local copies, waits for them, and re-layouts  4.41 us (7%)
    pallas_call x1, Pallas kernels, per_device(): pl.pallas_call(functools.partial(kernel, slabs, subs, cx, cy, nz), out_sh...  61.3 us
    unnamed x7, local copies, waits for them, and re-layouts  4.41 us

commit v1 on v0

v1 whole, which is shorter than its diff:
```python
import functools

import jax
import jax.numpy as jnp
from jax import lax
from jax.experimental import pallas as pl
from jax.experimental.pallas import tpu as pltpu
from jax.sharding import PartitionSpec as P

ITERS = 3
UNROLL = 3
LANES = 128
MESH = pl.DeviceIdType.MESH


def fold(x):
    rows, cols = x.shape
    total = None
    for r in range(0, rows, 8):
        for c in range(0, cols, LANES):
            piece = x[r : r + 8, c : c + LANES]
            total = piece if total is None else total + piece
    return total


def loop(count, body, init=0, low=0):
    step = max(u for u in range(1, UNROLL + 1) if count % u == 0)

    def several(k, carry):
        for i in range(step):
            carry = body(low + k * step + i, carry)
        return carry

    return lax.fori_loop(0, count // step, several, init)


def kernel(
    slabs, subs, cx, cy, nz,
    start, wind, reaction, mass, ob, os_, scal,
    stage, xp, xu, qs, y0, t1, z1, raw, co, mk, vv, ss, wl, red,
    init_send, init_recv, send, recv, red_send, red_recv, load, out_local, out_send, out_recv,
):
    slab, sub = lax.axis_index("slab"), lax.axis_index("sub")
    n = slabs * subs
    me = slab * subs + sub
    h = cx // subs
    rows = subs * cy
    f32 = jnp.float32
    other = 1 - sub
    has_left, has_right = me > 0, me < n - 1
    has_cross = jnp.where(sub == 0, slab, slabs - 1 - slab) > 0
    mine = pl.ds(pl.multiple_of(sub * cy, 8), cy)
    theirs = pl.ds(pl.multiple_of(other * cy, 8), cy)

    def staged(lo, count):
        return lambda planes: stage.at[pl.ds(lo, count), planes]

    first = [
        (lambda planes: stage.at[3, planes], lambda planes, lines: xp.at[0, planes, lines], 2, 2),
        (staged(4, 4), lambda planes, lines: raw.at[pl.ds(0, 4), planes, lines], 1, 1),
        (lambda planes: stage.at[8, planes], lambda planes, lines: raw.at[4, planes, lines], 1, 0),
        (staged(0, 3), lambda planes, lines: xu.at[0, :, planes, lines], 1, 1),
    ]

    def window(g, side):
        _, _, at, w = first[g]
        return pl.ds(side * (h - w), h + w), pl.ds(at - side * w, h + w)

    def local(g, src, dst, sem):
        a, b = window(g, sub)
        return pltpu.make_async_copy(src(a), dst(b), load.at[sem])

    stages = [
        pltpu.make_async_copy(start.at[3], stage.at[3], load.at[0]),
        pltpu.make_async_copy(wind, stage.at[pl.ds(4, 3)], load.at[1]),
        pltpu.make_async_copy(reaction, stage.at[7], load.at[2]),
        pltpu.make_async_copy(mass, stage.at[8], load.at[3]),
        pltpu.make_async_copy(start.at[pl.ds(0, 3)], stage.at[pl.ds(0, 3)], load.at[4]),
    ]
    own = [
        local(0, lambda a: start.at[3, a], lambda b: xp.at[0, b, mine], 5),
        local(1, lambda a: wind.at[:, a], lambda b: raw.at[pl.ds(0, 3), b, mine], 6),
        local(1, lambda a: reaction.at[a], lambda b: raw.at[3, b, mine], 7),
        local(2, lambda a: mass.at[a], lambda b: raw.at[4, b, mine], 8),
        local(3, lambda a: start.at[pl.ds(0, 3), a], lambda b: xu.at[0, :, b, mine], 9),
    ]
    first_out = pltpu.make_async_copy(start, ob.at[0], load.at[10])
    for item in stages:
        item.start()
    for item in own:
        item.start()
    first_out.start()

    barrier = pltpu.get_barrier_semaphore()

    def greet(k, carry):
        for core in range(subs):
            pl.semaphore_signal(
                barrier, inc=1, device_id=(lax.rem(slab + k, slabs), core), device_id_type=MESH
            )
        return carry

    pl.semaphore_signal(barrier, inc=1, device_id=(slab, other), device_id_type=MESH)
    lax.fori_loop(1, slabs, greet, 0)

    def clear(low):
        def inner():
            zero = jnp.zeros((rows, nz), f32)
            for e in range(ITERS):
                for k in range(2):
                    at = k if low else 2 + h + k
                    xp[e, at] = zero
                    qs[e, at] = zero
                for c in range(3):
                    xu[e, c, 0 if low else 1 + h] = zero
                    y0[e, c, 0 if low else 3 + h] = zero
            for c in range(4):
                raw[c, 0 if low else 1 + h] = zero
        return inner

    pl.when(jnp.logical_not(has_left))(clear(True))
    pl.when(jnp.logical_not(has_right))(clear(False))

    row = lax.broadcasted_iota(jnp.int32, (rows, nz), 0)
    col = lax.broadcasted_iota(jnp.int32, (rows, nz), 1)
    mk[0] = jnp.where(row == rows - 1, 0.0, 1.0)
    mk[1] = jnp.where(row == 0, 0.0, 1.0)
    mk[2] = jnp.where(col == nz - 1, 0.0, 1.0)
    mk[3] = jnp.where(col == 0, 0.0, 1.0)

    def first_copy(g, kind):
        src, dst, at, w = first[g]
        if kind == 0:
            a, b = window(g, other)
            target, slot = (slab, other), 0
        elif kind == 1:
            a, b = pl.ds(cx - w, w), pl.ds(at - w, w)
            target, slot = (slab + 1, 0), 1 + sub
        else:
            a, b = pl.ds(0, w), pl.ds(at + h, w)
            target, slot = (slab - 1, subs - 1), 1 + sub
        return pltpu.make_async_remote_copy(
            src_ref=src(a), dst_ref=dst(b, mine), send_sem=init_send.at[g, kind],
            recv_sem=init_recv.at[g, slot], device_id=target, device_id_type=MESH,
        )

    def first_begin(g):
        if first[g][3] > 0:
            pl.when(slab < slabs - 1)(lambda: first_copy(g, 1).start())
            pl.when(slab > 0)(lambda: first_copy(g, 2).start())

    def first_wait(ref, sem):
        pltpu.make_async_copy(ref, ref, sem).wait()

    def first_near(g):
        _, dst, _, _ = first[g]
        _, b = window(g, sub)
        first_wait(dst(b, theirs), init_recv.at[g, 0])

    def first_far(g):
        _, dst, at, w = first[g]
        if w > 0:
            def inner():
                for r in range(subs):
                    first_wait(dst(pl.ds(0, w), pl.ds(r * cy, cy)), init_recv.at[g, 1 + r])
            pl.when(has_cross)(inner)

    def first_finish(g):
        first_copy(g, 0).wait_send()
        if first[g][3] > 0:
            pl.when(slab < slabs - 1)(lambda: first_copy(g, 1).wait_send())
            pl.when(slab > 0)(lambda: first_copy(g, 2).wait_send())

    def remote(kind, e, way):
        if kind == 0 or kind == 2:
            ref = (xp, None, qs)[kind].at[e]
            pair = (pl.ds(h, 2), pl.ds(0, 2)) if way == 0 else (pl.ds(2, 2), pl.ds(h + 2, 2))
            src, dst = ref.at[pair[0]], ref.at[pair[1]]
        elif kind == 1:
            pair = (h, 0) if way == 0 else (1, h + 1)
            src, dst = xu.at[e, :, pair[0]], xu.at[e, :, pair[1]]
        else:
            pair = (h, 0) if way == 0 else (3, h + 3)
            src, dst = y0.at[e, :, pair[0]], y0.at[e, :, pair[1]]
        target = me + 1 if way == 0 else me - 1
        return pltpu.make_async_remote_copy(
            src_ref=src, dst_ref=dst, send_sem=send.at[kind, e, way], recv_sem=recv.at[kind, e, way],
            device_id=(target // subs, lax.rem(target, subs)), device_id_type=MESH,
        )

    def begin(kind, e):
        pl.when(has_right)(lambda: remote(kind, e, 0).start())
        pl.when(has_left)(lambda: remote(kind, e, 1).start())

    def arrive(kind, e):
        pl.when(has_left)(lambda: remote(kind, e, 0).wait_recv())
        pl.when(has_right)(lambda: remote(kind, e, 1).wait_recv())

    def finish(kind, e):
        pl.when(has_right)(lambda: remote(kind, e, 0).wait_send())
        pl.when(has_left)(lambda: remote(kind, e, 1).wait_send())

    lane = lax.broadcasted_iota(jnp.int32, (1, LANES), 1)

    def reduce_start(e, parts):
        line = jnp.zeros((1, LANES), f32)
        for i, part in enumerate(parts):
            line = line + jnp.where(lane == i, jnp.sum(fold(part), keepdims=True), 0.0)
        red[e, me] = line

        def tell(at, core):
            pltpu.make_async_remote_copy(
                src_ref=red.at[e, me], dst_ref=red.at[e, me],
                send_sem=red_send.at[e], recv_sem=red_recv.at[e],
                device_id=(at, core), device_id_type=MESH,
            ).start()

        def push(k, carry):
            at = lax.rem(slab + k, slabs)
            for core in range(subs):
                tell(at, core)
            return carry

        lax.fori_loop(1, slabs, push, 0)
        tell(slab, other)

    def red_wait(e, sem):
        block = red.at[e, pl.ds(0, n - 1)]
        pltpu.make_async_copy(block, block, sem.at[e]).wait()

    def reduce_end(e, count):
        red_wait(e, red_recv)
        total = jnp.sum(red[e], axis=0)
        return [
            jnp.sum(jnp.where(lane == i, total, 0.0), axis=1, keepdims=True)
            for i in range(count)
        ]

    def deliver(i, src, dst):
        planes = pl.ds(sub * h, h)
        return (
            pltpu.make_async_copy(src.at[:, :, mine], dst.at[:, planes], out_local.at[i]),
            pltpu.make_async_remote_copy(
                src_ref=src.at[:, :, theirs], dst_ref=dst.at[:, planes],
                send_sem=out_send.at[i], recv_sem=out_recv.at[i],
                device_id=(slab, other), device_id_type=MESH,
            ),
        )

    def results():
        return [deliver(e, ss.at[e], os_.at[e]) for e in range(ITERS)] + [
            deliver(ITERS + e, vv.at[e], ob.at[e + 1]) for e in range(ITERS - 1)
        ] + [deliver(2 * ITERS - 1, wl, ob.at[ITERS])]

    outs = results()

    def hand_over(i):
        for item in outs[i]:
            item.start()

    def turn(f):
        return (
            pltpu.roll(f, rows - 1, 0), pltpu.roll(f, 1, 0),
            pltpu.roll(f, nz - 1, 1), pltpu.roll(f, 1, 1),
        )

    def masked(f):
        yp, ym, zp, zm = turn(f)
        return yp * mk[0], ym * mk[1], zp * mk[2], zm * mk[3]

    def off_diagonal(below, around, above, k):
        yp, ym, zp, zm = around
        total = co[0, k] * above + co[1, k] * below
        total = total + (co[2, k] * yp + co[3, k] * ym)
        return total + (co[4, k] * zp + co[5, k] * zm)

    def inside(k):
        at = me * h + k
        return jnp.where(jnp.logical_and(at >= 0, at < n * h), 1.0, 0.0)

    def coefficients(k, carry):
        hx, hy, hz = 0.5 * raw[0, k], 0.5 * raw[1, k], 0.5 * raw[2, k]
        co[0, k] = 1.0 - hx
        co[1, k] = 1.0 + hx
        co[2, k] = (1.0 - hy) * mk[0]
        co[3, k] = (1.0 + hy) * mk[1]
        co[4, k] = (1.0 - hz) * mk[2]
        co[5, k] = (1.0 + hz) * mk[3]
        diagonal = 6.0 + raw[3, k]
        co[6, k] = diagonal
        co[7, k] = inside(k - 1) / diagonal
        return carry

    def masses(k, carry):
        co[8, k] = 1.0 / raw[4, k]
        return carry

    def guess(e):
        def body(k, carry):
            here = xp[e, k + 1]
            yp, ym, zp, zm = masked(here)
            total = (xp[e, k] + xp[e, k + 2]) + (yp + ym) + (zp + zm)
            t1[k] = (here + total * (1.0 / 7.0)) * (inside(k - 1) * (1.0 / 7.0))
            return carry
        return body

    def schur(e):
        def body(k, carry):
            here = t1[k + 1]
            off = off_diagonal(t1[k], turn(here), t1[k + 2], k + 1)
            qs[e, k + 2] = (off - co[6, k + 1] * here) * co[8, k + 1]
            return carry
        return body

    def velocity_first(e):
        def body(k, carry):
            yp, ym, zp, zm = masked(qs[e, k + 2])
            scale = co[7, k + 1]
            y0[e, 0, k + 2] = (xu[e, 0, k + 1] - 0.5 * (qs[e, k + 3] - qs[e, k + 1])) * scale
            y0[e, 1, k + 2] = (xu[e, 1, k + 1] - 0.5 * (yp - ym)) * scale
            y0[e, 2, k + 2] = (xu[e, 2, k + 1] - 0.5 * (zp - zm)) * scale
            return carry
        return body

    def velocity_second(e):
        def body(k, carry):
            for c in range(3):
                here = y0[e, c, k + 2]
                off = off_diagonal(y0[e, c, k + 1], turn(here), y0[e, c, k + 3], k + 1)
                z1[c, k + 1] = off * co[7, k + 1]
            return carry
        return body

    def image(e, factor, weights):
        def mix(value, held):
            if e > 0:
                value = value * factor
                for g, item in zip(weights, held):
                    value = value - g * item
            return value

        def body(k, carry):
            q = qs[e, k + 2]
            qa, qb = qs[e, k + 3], qs[e, k + 1]
            yp, ym, zp, zm = masked(q)
            low = 0.5 * ((qa + qb) + (yp + ym) + (zp + zm)) - 3.0 * q
            for c in range(3):
                here = z1[c, k + 1]
                off = off_diagonal(z1[c, k], turn(here), z1[c, k + 2], k + 1)
                value = mix(xu[e, c, k + 1] - off, [xu[i + 1, c, k + 1] for i in range(e)])
                full = y0[e, c, k + 2] + here
                if c == 0:
                    above = y0[e, 0, k + 3] + z1[0, k + 2]
                    below = y0[e, 0, k + 1] + z1[0, k]
                    low = low - 0.5 * (above - below)
                elif c == 1:
                    a, b = pltpu.roll(full, rows - 1, 0), pltpu.roll(full, 1, 0)
                    low = low - 0.5 * (a * mk[0] - b * mk[1])
                else:
                    a, b = pltpu.roll(full, nz - 1, 1), pltpu.roll(full, 1, 1)
                    low = low - 0.5 * (a * mk[2] - b * mk[3])
                ss[e, c, k] = mix(full, [ss[i, c, k] for i in range(e)])
                if e + 1 < ITERS:
                    xu[e + 1, c, k + 1] = value
                else:
                    wl[c, k] = value
            ss[e, 3, k] = mix(q, [ss[i, 3, k] for i in range(e)])
            value = mix(low, [xp[i + 1, k + 2] for i in range(e)])
            if e + 1 < ITERS:
                xp[e + 1, k + 2] = value
            else:
                wl[3, k] = value
            return carry
        return body

    def held_of(i, c, k):
        if i > 0:
            return vv[i - 1, c, k]
        return xp[0, k + 2] if c == 3 else xu[0, c, k + 1]

    def image_of(e, c, k):
        if e + 1 == ITERS:
            return wl[c, k]
        return xp[e + 1, k + 2] if c == 3 else xu[e + 1, c, k + 1]

    stages[0].wait()
    pl.semaphore_wait(barrier, n - 1)
    first_begin(0)
    first_copy(0, 0).start()
    for item in stages[1:4]:
        item.wait()
    first_begin(1)
    first_copy(1, 0).start()
    first_copy(2, 0).start()
    stages[4].wait()
    first_begin(3)
    first_copy(3, 0).start()
    for item in own[1:4]:
        item.wait()
    first_near(1)
    first_near(2)
    loop(h, coefficients, low=1)
    loop(h, masses, low=1)
    own[0].wait()
    first_near(0)
    first_far(0)

    zero = jnp.zeros((rows, nz), f32)
    inverses, entries = [], {}
    factor, weights = None, []
    for e in range(ITERS):
        if e > 0:
            arrive(0, e)
        loop(h + 2, guess(e))
        loop(h, schur(e))
        begin(2, e)
        if e == 0:
            own[4].wait()
            first_near(3)
        loop(h - 2, velocity_first(e), low=1)
        begin(3, e)
        if e == 0:
            first_far(1)
            coefficients(0, 0)
            coefficients(h + 1, 0)
            first_far(3)
        else:
            sums = reduce_end(e - 1, e + 1)
            norm = jnp.sqrt(sums[0])
            factor = 1.0 / norm
            if e > 1:
                entries[(e - 1, e - 2)] = norm
            inverses.append(factor)
            weights = []
            for i in range(e):
                value = sums[i + 1] * inverses[i] * factor
                entries[(i, e - 1)] = value
                weights.append(value * inverses[i])

            def form(k, carry, e=e):
                for c in range(4):
                    value = image_of(e - 1, c, k) * factor
                    for i in range(e):
                        value = value - weights[i] * held_of(i, c, k)
                    vv[e - 1, c, k] = value
                return carry

            loop(h, form)
            hand_over(ITERS + e - 1)
            arrive(1, e)
        arrive(2, e)
        for k in (0, h - 1, -1, h):
            velocity_first(e)(k, 0)
        loop(h, velocity_second(e))
        for c in range(3):
            z1[c, 0] = zero
            z1[c, h + 1] = zero
        loop(h, image(e, factor, weights))
        hand_over(e)
        arrive(3, e)

        scale = factor if e > 0 else 1.0

        def patch(c, e=e, scale=scale):
            low, high = [], []
            for k, found in ((-1, low), (h, high)):
                here = y0[e, c, k + 2]
                off = off_diagonal(y0[e, c, k + 1], turn(here), y0[e, c, k + 3], k + 1)
                found.append(off * co[7, k + 1] * scale)
            low, high = low[0], high[0]
            if e + 1 < ITERS:
                if c == 0:
                    xp[e + 1, 2] = xp[e + 1, 2] + 0.5 * low
                    xp[e + 1, h + 1] = xp[e + 1, h + 1] - 0.5 * high
                xu[e + 1, c, 1] = xu[e + 1, c, 1] - co[1, 1] * low
                xu[e + 1, c, h] = xu[e + 1, c, h] - co[0, h] * high
            else:
                if c == 0:
                    wl[3, 0] = wl[3, 0] + 0.5 * low
                    wl[3, h - 1] = wl[3, h - 1] - 0.5 * high
                wl[c, 0] = wl[c, 0] - co[1, 1] * low
                wl[c, h - 1] = wl[c, h - 1] - co[0, h] * high

        patch(0)
        if e + 1 < ITERS:
            begin(0, e + 1)
        patch(1)
        patch(2)
        if e + 1 == ITERS:
            hand_over(2 * ITERS - 1)

        def totals(k, acc, e=e):
            acc = list(acc)
            found = [image_of(e, c, k) for c in range(4)]
            for i in range(e + 1):
                held = [held_of(i, c, k) for c in range(4)]
                term = held[0] * found[0] + held[1] * found[1]
                acc[i + 1] = acc[i + 1] + (term + (held[2] * found[2] + held[3] * found[3]))
                if i == e:
                    term = held[0] * held[0] + held[1] * held[1]
                    acc[0] = acc[0] + (term + (held[2] * held[2] + held[3] * held[3]))
            if e + 1 == ITERS:
                term = found[0] * found[0] + found[1] * found[1]
                acc[e + 2] = acc[e + 2] + (term + (found[2] * found[2] + found[3] * found[3]))
            return tuple(acc)

        count = e + 2 if e + 1 < ITERS else e + 3
        reduce_start(e, loop(h, totals, (zero,) * count))
        if e + 1 < ITERS:
            begin(1, e + 1)

    for g in range(len(first)):
        first_finish(g)
    first_out.wait()
    for e in range(ITERS):
        for kind in range(4):
            if e > 0 or kind > 1:
                finish(kind, e)
    for here, there in outs:
        here.wait()
        there.wait()
    for e in range(ITERS - 1):
        red_wait(e, red_send)
    sums = reduce_end(ITERS - 1, ITERS + 2)
    norm = jnp.sqrt(sums[0])
    factor = 1.0 / norm
    entries[(ITERS - 1, ITERS - 2)] = norm
    inverses.append(factor)
    left = sums[ITERS + 1] * factor * factor
    spread = []
    for i in range(ITERS):
        value = sums[i + 1] * inverses[i] * factor
        entries[(i, ITERS - 1)] = value
        spread.append(value * inverses[i])
        left = left - value * value
    norm = jnp.sqrt(left)
    entries[(ITERS, ITERS - 1)] = norm
    inverse = 1.0 / norm
    lines = inverses + [factor * inverse] + [g * inverse for g in spread]
    for i, value in enumerate(lines):
        scal[i : i + 1] = jnp.broadcast_to(value, (1, LANES))
    r = lax.broadcasted_iota(jnp.int32, (8, LANES), 0)
    c = lax.broadcasted_iota(jnp.int32, (8, LANES), 1)
    table = jnp.zeros((8, LANES), f32)
    for (i, j), value in entries.items():
        table = table + jnp.where(jnp.logical_and(r == i, c == j), value, 0.0)
    scal[8:16] = table
    red_wait(ITERS - 1, red_send)


def write(ob, os_, scal, basis, search, hess, bb, sb, hb, sems):
    def value(i):
        return scal[i : i + 1, 0:1]

    copies = []

    def emit(src, dst, i):
        item = pltpu.make_async_copy(src, dst, sems.at[i])
        item.start()
        copies.append(item)

    hb[...] = scal[8 : 8 + ITERS + 1, 0:ITERS]
    emit(hb, hess, 2 * ITERS + 1)
    planes = ob.shape[2]
    inverse = [value(i) for i in range(ITERS)]
    for e in range(ITERS):
        def body(k, carry, e=e):
            for c in range(4):
                bb[e, c, k] = ob[e, c, k] * inverse[e]
                sb[e, c, k] = os_[e, c, k] * inverse[e]
            return carry

        loop(planes, body)
        emit(bb.at[e], basis.at[e], e)
        emit(sb.at[e], search.at[e], ITERS + 1 + e)
    weights = [value(ITERS + i) for i in range(ITERS + 1)]

    def last(k, carry):
        for c in range(4):
            total = ob[ITERS, c, k] * weights[0]
            for i in range(ITERS):
                total = total - weights[i + 1] * ob[i, c, k]
            bb[ITERS, c, k] = total
        return carry

    loop(planes, last)
    emit(bb.at[ITERS], basis.at[ITERS], ITERS)
    for item in copies:
        item.wait()


def per_device(slabs, subs, start, wind, reaction, mass):
    _, cx, cy, nz = start.shape
    n = slabs * subs
    rows, h = subs * cy, cx // subs
    assert subs == 2 and cx % subs == 0 and h >= 3
    f32 = jnp.float32

    def field(*lead):
        return pltpu.VMEM((*lead, rows, nz), f32)

    anywhere = pl.BlockSpec(memory_space=pl.ANY)
    vmem = pl.BlockSpec(memory_space=pltpu.VMEM)
    hbm = pl.BlockSpec(memory_space=pltpu.HBM)
    ob, os_, scal = pl.pallas_call(
        functools.partial(kernel, slabs, subs, cx, cy, nz),
        out_shape=(
            jax.ShapeDtypeStruct((ITERS + 1, 4, cx, cy, nz), f32),
            jax.ShapeDtypeStruct((ITERS, 4, cx, cy, nz), f32),
            jax.ShapeDtypeStruct((16, LANES), f32),
        ),
        in_specs=[hbm] * 4,
        out_specs=(anywhere, anywhere, vmem),
        scratch_shapes=[
            pltpu.VMEM((9, cx, cy, nz), f32),
            field(ITERS, h + 4),
            field(ITERS, 3, h + 2),
            field(ITERS, h + 4),
            field(ITERS, 3, h + 4),
            field(h + 2),
            field(3, h + 2),
            field(5, h + 2),
            field(9, h + 2),
            field(4),
            field(ITERS - 1, 4, h),
            field(ITERS, 4, h),
            field(4, h),
            pltpu.VMEM((ITERS, n, 1, LANES), f32),
            pltpu.SemaphoreType.DMA((4, 3)),
            pltpu.SemaphoreType.DMA((4, 3)),
            pltpu.SemaphoreType.DMA((4, ITERS, 2)),
            pltpu.SemaphoreType.DMA((4, ITERS, 2)),
            pltpu.SemaphoreType.DMA((ITERS,)),
            pltpu.SemaphoreType.DMA((ITERS,)),
            pltpu.SemaphoreType.DMA((11,)),
            pltpu.SemaphoreType.DMA((2 * ITERS,)),
            pltpu.SemaphoreType.DMA((2 * ITERS,)),
            pltpu.SemaphoreType.DMA((2 * ITERS,)),
        ],
        compiler_params=pltpu.CompilerParams(
            collective_id=0, has_side_effects=True, vmem_limit_bytes=40_000_000
        ),
    )(start, wind, reaction, mass)
    return pl.pallas_call(
        write,
        out_shape=(
            jax.ShapeDtypeStruct((ITERS + 1, 4, cx, cy, nz), f32),
            jax.ShapeDtypeStruct((ITERS, 4, cx, cy, nz), f32),
            jax.ShapeDtypeStruct((ITERS + 1, ITERS), f32),
        ),
        in_specs=[vmem] * 3,
        out_specs=(hbm, hbm, hbm),
        scratch_shapes=[
            pltpu.VMEM((ITERS + 1, 4, cx, cy, nz), f32),
            pltpu.VMEM((ITERS, 4, cx, cy, nz), f32),
            pltpu.VMEM((ITERS + 1, ITERS), f32),
            pltpu.SemaphoreType.DMA((2 * ITERS + 2,)),
        ],
        compiler_params=pltpu.CompilerParams(vmem_limit_bytes=10_000_000),
    )(ob, os_, scal)


def solution(mesh):
    slabs, subs = mesh.shape["slab"], mesh.shape["sub"]
    return jax.shard_map(
        functools.partial(per_device, slabs, subs),
        mesh=mesh,
        in_specs=(
            P(None, "slab", "sub", None),
            P(None, "slab", "sub", None),
            P("slab", "sub", None),
            P("slab", "sub", None),
        ),
        out_specs=(P(None, None, "slab", "sub", None), P(None, None, "slab", "sub", None), P()),
        check_vma=False,
    )
```

time: 66.5 us -> 50 us (0.75)
  Pallas kernels: 61.3 us -> 45.4 us
  local copies, waits for them, and re-layouts: 4.41 us -> 3.73 us
    pallas_call x1, Pallas kernels: 61.3 us -> 43.7 us  [per_device(): pl.pallas_call(functools.partial(kernel, slabs, subs, cx, cy, nz), out_sh...]
    pallas_call x0 -> x1, Pallas kernels: none -> 1.71 us  [per_device(): pl.pallas_call(write, out_shape=(jax.ShapeDtypeStruct((ITERS + 1, 4, cx,...]
    unnamed x7 -> x8, local copies, waits for them, and re-layouts: 4.41 us -> 3.73 us
where the time goes in v1:
time: 50 us; the launch traced here: 49.8 us
  Pallas kernels  45.4 us (91%)
  local copies, waits for them, and re-layouts  3.73 us (7%)
  between operations  0.65 us (1%)
    pallas_call x1, Pallas kernels, per_device(): pl.pallas_call(functools.partial(kernel, slabs, subs, cx, cy, nz), out_sh...  43.7 us
    unnamed x8, local copies, waits for them, and re-layouts  3.73 us
    pallas_call x1, Pallas kernels, per_device(): pl.pallas_call(write, out_shape=(jax.ShapeDtypeStruct((ITERS + 1, 4, cx,...  1.71 us

profile of v1, /device:TPU:0, one launch (start us, length us, event | category | flops | bytes accessed | tf_op | source)
XLA Modules:
  0.0 49.8 jit_solution(17077342449885446569)
XLA Ops:
  0.6 0.0 copy-start
  0.6 1.0 %copy-done = f32[4,6,16,256]{3,2,1,0:T(8,128)S(1)} copy-done((f32[4,6,16,256]{3,2,1,0:T(8,128)S(1)}, f32[4,6,16,256]{3,2,1,0:T(8,128)}, u32[]{:S(2)}) %copy-start) | copy-done | bytes 393240
  1.6 0.0 copy-start.1
  1.6 1.0 %copy-done.1 = f32[3,6,16,256]{3,2,1,0:T(8,128)S(1)} copy-done((f32[3,6,16,256]{3,2,1,0:T(8,128)S(1)}, f32[3,6,16,256]{3,2,1,0:T(8,128)}, u32[]{:S(2)}) %copy-start.1) | copy-done | bytes 294936
  2.6 0.0 copy-start.2
  2.6 0.9 %copy-done.2 = f32[6,16,256]{2,1,0:T(8,128)S(1)} copy-done((f32[6,16,256]{2,1,0:T(8,128)S(1)}, f32[6,16,256]{2,1,0:T(8,128)}, u32[]{:S(2)}) %copy-start.2) | copy-done | bytes 98328
  3.5 0.0 copy-start.3
  3.5 0.9 %copy-done.3 = f32[6,16,256]{2,1,0:T(8,128)S(1)} copy-done((f32[6,16,256]{2,1,0:T(8,128)S(1)}, f32[6,16,256]{2,1,0:T(8,128)}, u32[]{:S(2)}) %copy-start.3) | copy-done | bytes 98328
  4.4 43.7 %shard_map.67 = (f32[4,4,6,16,256]{4,3,2,1,0:T(8,128)S(1)}, f32[3,4,6,16,256]{4,3,2,1,0:T(8,128)S(1)}, f32[16,128]{1,0:T(8,128)S(1)}) custom-call(f32[4,6,16,256]{3,2,1,0:T(8,128)S(1)} %copy-done, f32[3,6,16,256]{3,2,1,0:T(8,128)S(1)} %copy-done.1, f32[6,16,256]{2,1,0:T(8,128)S(1)} %copy-done.2, f32[6,16,256]{2,1,0:T(8,128)S(1)} %copy-done.3), custom_call_target="tpu_custom_call" | custom-call | tf_op jit(solution)/shard_map/pallas_call | solution.py:605
  48.1 1.7 %shard_map.68 = (f32[4,4,6,16,256]{4,3,2,1,0:T(8,128)}, f32[3,4,6,16,256]{4,3,2,1,0:T(8,128)}, f32[4,3]{1,0:T(4,128)}) custom-call(f32[4,4,6,16,256]{4,3,2,1,0:T(8,128)S(1)} %get-tuple-element.6.ob, f32[3,4,6,16,256]{4,3,2,1,0:T(8,128)S(1)} %get-tuple-element.7.os_, f32[16,128]{1,0:T(8,128)S(1)} %get-tuple-element.8.scal), custom_call_target="tpu_custom_call" | custom-call | tf_op jit(solution)/shard_map/pallas_call | solution.py:644
Async XLA Ops:
  0.6 1.0 %copy-start = (f32[4,6,16,256]{3,2,1,0:T(8,128)S(1)}, f32[4,6,16,256]{3,2,1,0:T(8,128)}, u32[]{:S(2)}) copy-start(f32[4,6,16,256]{3,2,1,0:T(8,128)} %start.1) | copy-start | bytes 1179652
  1.6 1.0 %copy-start.1 = (f32[3,6,16,256]{3,2,1,0:T(8,128)S(1)}, f32[3,6,16,256]{3,2,1,0:T(8,128)}, u32[]{:S(2)}) copy-start(f32[3,6,16,256]{3,2,1,0:T(8,128)} %wind.1) | copy-start | bytes 884740
  2.6 0.9 %copy-start.2 = (f32[6,16,256]{2,1,0:T(8,128)S(1)}, f32[6,16,256]{2,1,0:T(8,128)}, u32[]{:S(2)}) copy-start(f32[6,16,256]{2,1,0:T(8,128)} %reaction.1) | copy-start | bytes 294916
  3.5 0.9 %copy-start.3 = (f32[6,16,256]{2,1,0:T(8,128)S(1)}, f32[6,16,256]{2,1,0:T(8,128)}, u32[]{:S(2)}) copy-start(f32[6,16,256]{2,1,0:T(8,128)} %mass.1) | copy-start | bytes 294916

commit v2 on v1

--- a/solution.py
+++ b/solution.py
@@ -8,7 +8,7 @@
 from jax.sharding import PartitionSpec as P
 
 ITERS = 3
-UNROLL = 3
+UNROLL = 5
 LANES = 128
 MESH = pl.DeviceIdType.MESH
 
@@ -38,7 +38,7 @@
     slabs, subs, cx, cy, nz,
     start, wind, reaction, mass, ob, os_, scal,
     stage, xp, xu, qs, y0, t1, z1, raw, co, mk, vv, ss, wl, red,
-    init_send, init_recv, send, recv, red_send, red_recv, load, out_local, out_send, out_recv,
+    init_send, init_recv, send, recv, red_send, red_recv, load, out_local, out_send, out_recv, known,
 ):
     slab, sub = lax.axis_index("slab"), lax.axis_index("sub")
     n = slabs * subs
@@ -93,15 +93,38 @@
 
     barrier = pltpu.get_barrier_semaphore()
 
-    def greet(k, carry):
+    def greet(sem, at, core):
+        pl.semaphore_signal(sem, inc=1, device_id=(at, core), device_id_type=MESH)
+
+    def near(way):
         for core in range(subs):
-            pl.semaphore_signal(
-                barrier, inc=1, device_id=(lax.rem(slab + k, slabs), core), device_id_type=MESH
-            )
-        return carry
-
-    pl.semaphore_signal(barrier, inc=1, device_id=(slab, other), device_id_type=MESH)
-    lax.fori_loop(1, slabs, greet, 0)
+            greet(barrier, slab + way, core)
+
+    greet(barrier, slab, other)
+    pl.when(slab > 0)(lambda: near(-1))
+    pl.when(slab < slabs - 1)(lambda: near(1))
+    met = 1 + jnp.where(slab > 0, subs, 0) + jnp.where(slab < slabs - 1, subs, 0)
+    steps = [1 << i for i in range((slabs - 1).bit_length())]
+
+    def spread(i):
+        d = steps[i]
+        pl.when(slab + d < slabs)(lambda: greet(known.at[i, 0], slab + d, sub))
+        pl.when(slab - d >= 0)(lambda: greet(known.at[i, 1], slab - d, sub))
+
+    def gather(i):
+        d = steps[i]
+        pl.when(slab - d >= 0)(lambda: pl.semaphore_wait(known.at[i, 0], 1))
+        pl.when(slab + d < slabs)(lambda: pl.semaphore_wait(known.at[i, 1], 1))
+
+    def further(count):
+        for _ in range(count):
+            if pending:
+                i = pending.pop(0)
+                gather(i)
+                if i + 1 < len(steps):
+                    spread(i + 1)
+
+    pending = list(range(len(steps)))
 
     def clear(low):
         def inner():
@@ -384,9 +407,10 @@
         return xp[e + 1, k + 2] if c == 3 else xu[e + 1, c, k + 1]
 
     stages[0].wait()
-    pl.semaphore_wait(barrier, n - 1)
+    pl.semaphore_wait(barrier, met)
     first_begin(0)
     first_copy(0, 0).start()
+    spread(0)
     for item in stages[1:4]:
         item.wait()
     first_begin(1)
@@ -401,6 +425,7 @@
     first_near(2)
     loop(h, coefficients, low=1)
     loop(h, masses, low=1)
+    further(1)
     own[0].wait()
     first_near(0)
     first_far(0)
@@ -415,6 +440,7 @@
         loop(h, schur(e))
         begin(2, e)
         if e == 0:
+            further(1)
             own[4].wait()
             first_near(3)
         loop(h - 2, velocity_first(e), low=1)
@@ -424,6 +450,7 @@
             coefficients(0, 0)
             coefficients(h + 1, 0)
             first_far(3)
+            further(1)
         else:
             sums = reduce_end(e - 1, e + 1)
             norm = jnp.sqrt(sums[0])
@@ -457,6 +484,8 @@
             z1[c, h + 1] = zero
         loop(h, image(e, factor, weights))
         hand_over(e)
+        if e == 0:
+            further(len(steps))
         arrive(3, e)
 
         scale = factor if e > 0 else 1.0
@@ -636,11 +665,12 @@
             pltpu.SemaphoreType.DMA((2 * ITERS,)),
             pltpu.SemaphoreType.DMA((2 * ITERS,)),
             pltpu.SemaphoreType.DMA((2 * ITERS,)),
+            pltpu.SemaphoreType.REGULAR(((slabs - 1).bit_length(), 2)),
         ],
         compiler_params=pltpu.CompilerParams(
             collective_id=0, has_side_effects=True, vmem_limit_bytes=40_000_000
         ),
-    )(start, wind, reaction, mass)
+    )(*(pltpu.with_memory_space_constraint(x, pltpu.HBM) for x in (start, wind, reaction, mass)))
     return pl.pallas_call(
         write,
         out_shape=(

time: 50 us -> 43 us (0.86)
  local copies, waits for them, and re-layouts: 3.73 us -> 0 us
  Pallas kernels: 45.4 us -> 42.2 us
    unnamed x8 -> x0, local copies, waits for them, and re-layouts: 3.73 us -> none
    pallas_call x1, Pallas kernels: 43.7 us -> 40.5 us  [per_device(): pl.pallas_call(functools.partial(kernel, slabs, subs, cx, cy, nz), out_sh...]
where the time goes in v2:
time: 43 us; the launch traced here: 42.9 us
  Pallas kernels  42.2 us (98%)
  between operations  0.64 us (1%)
    pallas_call x1, Pallas kernels, per_device(): pl.pallas_call(functools.partial(kernel, slabs, subs, cx, cy, nz), out_sh...  40.5 us
    pallas_call x1, Pallas kernels, per_device(): pl.pallas_call(write, out_shape=(jax.ShapeDtypeStruct((ITERS + 1, 4, cx,...  1.71 us

profile of v2, /device:TPU:0, one launch (start us, length us, event | category | flops | bytes accessed | tf_op | source)
XLA Modules:
  0.0 42.9 jit_solution(1022259554515852361)
XLA Ops:
  0.6 40.5 %shard_map.67 = (f32[4,4,6,16,256]{4,3,2,1,0:T(8,128)S(1)}, f32[3,4,6,16,256]{4,3,2,1,0:T(8,128)S(1)}, f32[16,128]{1,0:T(8,128)S(1)}) custom-call(f32[4,6,16,256]{3,2,1,0:T(8,128)} %start.1, f32[3,6,16,256]{3,2,1,0:T(8,128)} %wind.1, f32[6,16,256]{2,1,0:T(8,128)} %reaction.1, f32[6,16,256]{2,1,0:T(8,128)} %mass.1), custom_call_target="tpu_custom_call" | custom-call | tf_op jit(solution)/shard_map/pallas_call | solution.py:634
  41.2 1.7 %shard_map.68 = (f32[4,4,6,16,256]{4,3,2,1,0:T(8,128)}, f32[3,4,6,16,256]{4,3,2,1,0:T(8,128)}, f32[4,3]{1,0:T(4,128)}) custom-call(f32[4,4,6,16,256]{4,3,2,1,0:T(8,128)S(1)} %get-tuple-element.6.ob, f32[3,4,6,16,256]{4,3,2,1,0:T(8,128)S(1)} %get-tuple-element.7.os_, f32[16,128]{1,0:T(8,128)S(1)} %get-tuple-element.8.scal), custom_call_target="tpu_custom_call" | custom-call | tf_op jit(solution)/shard_map/pallas_call | solution.py:674

commit v3 on v2

--- a/solution.py
+++ b/solution.py
@@ -37,7 +37,7 @@
 def kernel(
     slabs, subs, cx, cy, nz,
     start, wind, reaction, mass, ob, os_, scal,
-    stage, xp, xu, qs, y0, t1, z1, raw, co, mk, vv, ss, wl, red,
+    stage, xp, xu, qs, y0, yq, t1, z1, raw, co, ca, mk, vv, ss, wl, red,
     init_send, init_recv, send, recv, red_send, red_recv, load, out_local, out_send, out_recv, known,
 ):
     slab, sub = lax.axis_index("slab"), lax.axis_index("sub")
@@ -131,9 +131,9 @@
             zero = jnp.zeros((rows, nz), f32)
             for e in range(ITERS):
                 for k in range(2):
-                    at = k if low else 2 + h + k
-                    xp[e, at] = zero
-                    qs[e, at] = zero
+                    xp[e, k if low else 2 + h + k] = zero
+                qs[e, 1 if low else 2 + h] = zero
+                y0[e, 0, 1 if low else 2 + h] = zero
                 for c in range(3):
                     xu[e, c, 0 if low else 1 + h] = zero
                     y0[e, c, 0 if low else 3 + h] = zero
@@ -162,6 +162,9 @@
         else:
             a, b = pl.ds(0, w), pl.ds(at + h, w)
             target, slot = (slab - 1, subs - 1), 1 + sub
+        if kind > 0 and g == 3:
+            src = lambda planes: stage.at[pl.ds(1, 2), planes]
+            dst = lambda planes, lines: xu.at[0, pl.ds(1, 2), planes, lines]
         return pltpu.make_async_remote_copy(
             src_ref=src(a), dst_ref=dst(b, mine), send_sem=init_send.at[g, kind],
             recv_sem=init_recv.at[g, slot], device_id=target, device_id_type=MESH,
@@ -182,6 +185,8 @@
 
     def first_far(g):
         _, dst, at, w = first[g]
+        if g == 3:
+            dst = lambda planes, lines: xu.at[0, pl.ds(1, 2), planes, lines]
         if w > 0:
             def inner():
                 for r in range(subs):
@@ -195,16 +200,22 @@
             pl.when(slab > 0)(lambda: first_copy(g, 2).wait_send())
 
     def remote(kind, e, way):
-        if kind == 0 or kind == 2:
-            ref = (xp, None, qs)[kind].at[e]
-            pair = (pl.ds(h, 2), pl.ds(0, 2)) if way == 0 else (pl.ds(2, 2), pl.ds(h + 2, 2))
-            src, dst = ref.at[pair[0]], ref.at[pair[1]]
+        if kind == 0 or kind == 6:
+            deep = kind // 6
+            pair = (h + 1 - deep, 1 - deep) if way == 0 else (2 + deep, h + 2 + deep)
+            src, dst = xp.at[e, pair[0]], xp.at[e, pair[1]]
         elif kind == 1:
-            pair = (h, 0) if way == 0 else (1, h + 1)
-            src, dst = xu.at[e, :, pair[0]], xu.at[e, :, pair[1]]
+            pair, pick = (h, 0) if way == 0 else (1, h + 1), pl.ds(1, 2)
+            src, dst = xu.at[e, pick, pair[0]], xu.at[e, pick, pair[1]]
+        elif kind == 2:
+            pair = (h + 1, 1) if way == 0 else (2, h + 2)
+            src, dst = qs.at[e, pair[0]], qs.at[e, pair[1]]
+        elif kind == 4:
+            src, dst = yq.at[e, way], y0.at[e, 0, 1 if way == 0 else h + 2]
         else:
             pair = (h, 0) if way == 0 else (3, h + 3)
-            src, dst = y0.at[e, :, pair[0]], y0.at[e, :, pair[1]]
+            pick = 0 if kind == 3 else pl.ds(1, 2)
+            src, dst = y0.at[e, pick, pair[0]], y0.at[e, pick, pair[1]]
         target = me + 1 if way == 0 else me - 1
         return pltpu.make_async_remote_copy(
             src_ref=src, dst_ref=dst, send_sem=send.at[kind, e, way], recv_sem=recv.at[kind, e, way],
@@ -318,6 +329,23 @@
         co[8, k] = 1.0 / raw[4, k]
         return carry
 
+    def guess_own(e):
+        for k in range(1, h + 1):
+            here = xp[e, k + 1]
+            yp, ym, zp, zm = masked(here)
+            total = (yp + ym) + (zp + zm)
+            if k > 1:
+                total = total + xp[e, k]
+            if k < h:
+                total = total + xp[e, k + 2]
+            t1[k] = (here + total * (1.0 / 7.0)) * (1.0 / 7.0)
+
+    def guess_rest(e):
+        t1[1] = t1[1] + xp[e, 1] * (1.0 / 49.0)
+        t1[h] = t1[h] + xp[e, h + 2] * (1.0 / 49.0)
+        for k in (0, h + 1):
+            guess(e)(k, 0)
+
     def guess(e):
         def body(k, carry):
             here = xp[e, k + 1]
@@ -335,64 +363,118 @@
             return carry
         return body
 
-    def velocity_first(e):
+    def velocity_along(e, k):
+        found = xu[e, 0, k + 1] - 0.5 * (qs[e, k + 3] - qs[e, k + 1])
+        y0[e, 0, k + 2] = found * co[7, k + 1]
+
+    def velocity_across(e):
         def body(k, carry):
             yp, ym, zp, zm = masked(qs[e, k + 2])
             scale = co[7, k + 1]
-            y0[e, 0, k + 2] = (xu[e, 0, k + 1] - 0.5 * (qs[e, k + 3] - qs[e, k + 1])) * scale
             y0[e, 1, k + 2] = (xu[e, 1, k + 1] - 0.5 * (yp - ym)) * scale
             y0[e, 2, k + 2] = (xu[e, 2, k + 1] - 0.5 * (zp - zm)) * scale
             return carry
         return body
 
-    def velocity_second(e):
-        def body(k, carry):
-            for c in range(3):
-                here = y0[e, c, k + 2]
-                off = off_diagonal(y0[e, c, k + 1], turn(here), y0[e, c, k + 3], k + 1)
-                z1[c, k + 1] = off * co[7, k + 1]
-            return carry
-        return body
-
-    def image(e, factor, weights):
+    def second(e, c, k, skip=None):
+        yp, ym, zp, zm = turn(y0[e, c, k + 2])
+        off = (co[2, k + 1] * yp + co[3, k + 1] * ym) + (co[4, k + 1] * zp + co[5, k + 1] * zm)
+        if skip != 0:
+            off = off + co[0, k + 1] * y0[e, c, k + 3]
+        if skip != 1:
+            off = off + co[1, k + 1] * y0[e, c, k + 1]
+        z1[c, k + 1] = off * co[7, k + 1]
+
+    def second_across(e):
+        for c in (1, 2):
+            for k in range(h):
+                second(e, c, k, 1 if k == 0 else 0 if k == h - 1 else None)
+
+    def across(e, k):
+        one, two = y0[e, 1, k + 2] + z1[1, k + 1], y0[e, 2, k + 2] + z1[2, k + 1]
+        a, b = pltpu.roll(one, rows - 1, 0), pltpu.roll(one, 1, 0)
+        found = a * mk[0] - b * mk[1]
+        a, b = pltpu.roll(two, nz - 1, 1), pltpu.roll(two, 1, 1)
+        return 0.5 * (found + (a * mk[2] - b * mk[3]))
+
+    def low_own(e):
+        for k in range(h):
+            q = qs[e, k + 2]
+            yp, ym, zp, zm = masked(q)
+            total = (yp + ym) + (zp + zm)
+            if k > 0:
+                total = total + qs[e, k + 1]
+            if k < h - 1:
+                total = total + qs[e, k + 3]
+            total = 0.5 * total - 3.0 * q
+            if 0 < k < h - 1:
+                total = total - across(e, k)
+            t1[k + 1] = total
+
+    def velocity_share(e):
+        yq[e, 0] = (xu[e, 0, h] + 0.5 * qs[e, h]) * co[7, h]
+        yq[e, 1] = (xu[e, 0, 1] - 0.5 * qs[e, 3]) * co[7, 1]
+
+    def velocity_edges(e):
+        for k, near, sign in ((-1, 2, -0.5), (h, h + 1, 0.5)):
+            yp, ym, zp, zm = masked(qs[e, k + 2])
+            scale = co[7, k + 1]
+            y0[e, 0, k + 2] = y0[e, 0, k + 2] + (sign * qs[e, near]) * scale
+            y0[e, 1, k + 2] = (xu[e, 1, k + 1] - 0.5 * (yp - ym)) * scale
+            y0[e, 2, k + 2] = (xu[e, 2, k + 1] - 0.5 * (zp - zm)) * scale
+
+    def second_rest(e):
+        for c in (1, 2):
+            z1[c, 1] = z1[c, 1] + co[1, 1] * y0[e, c, 1] * co[7, 1]
+            z1[c, h] = z1[c, h] + co[0, h] * y0[e, c, h + 2] * co[7, h]
+        for k in range(h):
+            second(e, 0, k)
+        second_edges(e, 0)
+
+    def second_edges(e, c):
+        second(e, c, -1, 1)
+        second(e, c, h, 0)
+
+    def mixer(e, factor, weights):
         def mix(value, held):
             if e > 0:
                 value = value * factor
                 for g, item in zip(weights, held):
                     value = value - g * item
             return value
-
-        def body(k, carry):
-            q = qs[e, k + 2]
-            qa, qb = qs[e, k + 3], qs[e, k + 1]
-            yp, ym, zp, zm = masked(q)
-            low = 0.5 * ((qa + qb) + (yp + ym) + (zp + zm)) - 3.0 * q
-            for c in range(3):
-                here = z1[c, k + 1]
-                off = off_diagonal(z1[c, k], turn(here), z1[c, k + 2], k + 1)
-                value = mix(xu[e, c, k + 1] - off, [xu[i + 1, c, k + 1] for i in range(e)])
-                full = y0[e, c, k + 2] + here
-                if c == 0:
-                    above = y0[e, 0, k + 3] + z1[0, k + 2]
-                    below = y0[e, 0, k + 1] + z1[0, k]
-                    low = low - 0.5 * (above - below)
-                elif c == 1:
-                    a, b = pltpu.roll(full, rows - 1, 0), pltpu.roll(full, 1, 0)
-                    low = low - 0.5 * (a * mk[0] - b * mk[1])
-                else:
-                    a, b = pltpu.roll(full, nz - 1, 1), pltpu.roll(full, 1, 1)
-                    low = low - 0.5 * (a * mk[2] - b * mk[3])
-                ss[e, c, k] = mix(full, [ss[i, c, k] for i in range(e)])
-                if e + 1 < ITERS:
-                    xu[e + 1, c, k + 1] = value
-                else:
-                    wl[c, k] = value
-            ss[e, 3, k] = mix(q, [ss[i, 3, k] for i in range(e)])
+        return mix
+
+    def image_low(e, factor, weights):
+        mix = mixer(e, factor, weights)
+        full = [y0[e, 0, k + 2] + z1[0, k + 1] for k in range(-1, h + 1)]
+        for k in range(h):
+            low = t1[k + 1] - 0.5 * (full[k + 2] - full[k])
+            if k == 0:
+                low = low + 0.5 * qs[e, 1]
+            if k == h - 1:
+                low = low + 0.5 * qs[e, h + 2]
+            if k == 0 or k == h - 1:
+                low = low - across(e, k)
             value = mix(low, [xp[i + 1, k + 2] for i in range(e)])
             if e + 1 < ITERS:
                 xp[e + 1, k + 2] = value
             else:
                 wl[3, k] = value
+
+    def image(e, factor, weights):
+        mix = mixer(e, factor, weights)
+
+        def body(k, carry):
+            for c in range(3):
+                here = z1[c, k + 1]
+                off = off_diagonal(z1[c, k], turn(here), z1[c, k + 2], k + 1)
+                value = mix(xu[e, c, k + 1] - off, [xu[i + 1, c, k + 1] for i in range(e)])
+                ss[e, c, k] = mix(y0[e, c, k + 2] + here, [ss[i, c, k] for i in range(e)])
+                if e + 1 < ITERS:
+                    xu[e + 1, c, k + 1] = value
+                else:
+                    wl[c, k] = value
+            ss[e, 3, k] = mix(qs[e, k + 2], [ss[i, 3, k] for i in range(e)])
             return carry
         return body
 
@@ -428,6 +510,7 @@
     further(1)
     own[0].wait()
     first_near(0)
+    guess_own(0)
     first_far(0)
 
     zero = jnp.zeros((rows, nz), f32)
@@ -435,20 +518,32 @@
     factor, weights = None, []
     for e in range(ITERS):
         if e > 0:
+            arrive(6, e)
             arrive(0, e)
-        loop(h + 2, guess(e))
+        guess_rest(e)
         loop(h, schur(e))
         begin(2, e)
         if e == 0:
             further(1)
             own[4].wait()
             first_near(3)
-        loop(h - 2, velocity_first(e), low=1)
+        velocity_share(e)
+        begin(4, e)
+        for k in range(1, h - 1):
+            velocity_along(e, k)
         begin(3, e)
+        loop(h, velocity_across(e))
+        begin(5, e)
+        second_across(e)
+        low_own(e)
         if e == 0:
             first_far(1)
             coefficients(0, 0)
             coefficients(h + 1, 0)
+            ca[0] = co[1, 0] * co[7, 0]
+            ca[1] = co[0, h + 1] * co[7, h + 1]
+            ca[2] = co[1, 1] * ca[0]
+            ca[3] = co[0, h] * ca[1]
             first_far(3)
             further(1)
         else:
@@ -476,45 +571,44 @@
             hand_over(ITERS + e - 1)
             arrive(1, e)
         arrive(2, e)
-        for k in (0, h - 1, -1, h):
-            velocity_first(e)(k, 0)
-        loop(h, velocity_second(e))
-        for c in range(3):
-            z1[c, 0] = zero
-            z1[c, h + 1] = zero
+        velocity_along(e, 0)
+        velocity_along(e, h - 1)
+        arrive(4, e)
+        velocity_edges(e)
+        second_rest(e)
+        image_low(e, factor, weights)
+        if e + 1 < ITERS:
+            begin(6, e + 1)
+        arrive(3, e)
+
+        scale = factor if e > 0 else 1.0
+
+        def beyond(c, e=e, scale=scale):
+            return y0[e, c, 0] * scale, y0[e, c, h + 3] * scale
+
+        below, above = beyond(0)
+        if e + 1 < ITERS:
+            xp[e + 1, 2] = xp[e + 1, 2] + 0.5 * (ca[0] * below)
+            xp[e + 1, h + 1] = xp[e + 1, h + 1] - 0.5 * (ca[1] * above)
+            begin(0, e + 1)
+        else:
+            wl[3, 0] = wl[3, 0] + 0.5 * (ca[0] * below)
+            wl[3, h - 1] = wl[3, h - 1] - 0.5 * (ca[1] * above)
+        second_edges(e, 1)
+        second_edges(e, 2)
         loop(h, image(e, factor, weights))
         hand_over(e)
         if e == 0:
             further(len(steps))
-        arrive(3, e)
-
-        scale = factor if e > 0 else 1.0
-
-        def patch(c, e=e, scale=scale):
-            low, high = [], []
-            for k, found in ((-1, low), (h, high)):
-                here = y0[e, c, k + 2]
-                off = off_diagonal(y0[e, c, k + 1], turn(here), y0[e, c, k + 3], k + 1)
-                found.append(off * co[7, k + 1] * scale)
-            low, high = low[0], high[0]
+        arrive(5, e)
+        for c in range(3):
+            below, above = beyond(c)
             if e + 1 < ITERS:
-                if c == 0:
-                    xp[e + 1, 2] = xp[e + 1, 2] + 0.5 * low
-                    xp[e + 1, h + 1] = xp[e + 1, h + 1] - 0.5 * high
-                xu[e + 1, c, 1] = xu[e + 1, c, 1] - co[1, 1] * low
-                xu[e + 1, c, h] = xu[e + 1, c, h] - co[0, h] * high
+                xu[e + 1, c, 1] = xu[e + 1, c, 1] - ca[2] * below
+                xu[e + 1, c, h] = xu[e + 1, c, h] - ca[3] * above
             else:
-                if c == 0:
-                    wl[3, 0] = wl[3, 0] + 0.5 * low
-                    wl[3, h - 1] = wl[3, h - 1] - 0.5 * high
-                wl[c, 0] = wl[c, 0] - co[1, 1] * low
-                wl[c, h - 1] = wl[c, h - 1] - co[0, h] * high
-
-        patch(0)
-        if e + 1 < ITERS:
-            begin(0, e + 1)
-        patch(1)
-        patch(2)
+                wl[c, 0] = wl[c, 0] - ca[2] * below
+                wl[c, h - 1] = wl[c, h - 1] - ca[3] * above
         if e + 1 == ITERS:
             hand_over(2 * ITERS - 1)
 
@@ -537,13 +631,14 @@
         reduce_start(e, loop(h, totals, (zero,) * count))
         if e + 1 < ITERS:
             begin(1, e + 1)
+            guess_own(e + 1)
 
     for g in range(len(first)):
         first_finish(g)
     first_out.wait()
     for e in range(ITERS):
-        for kind in range(4):
-            if e > 0 or kind > 1:
+        for kind in range(7):
+            if e > 0 or kind in (2, 3, 4, 5):
                 finish(kind, e)
     for here, there in outs:
         here.wait()
@@ -646,10 +741,12 @@
             field(ITERS, 3, h + 2),
             field(ITERS, h + 4),
             field(ITERS, 3, h + 4),
+            field(ITERS, 2),
             field(h + 2),
             field(3, h + 2),
             field(5, h + 2),
             field(9, h + 2),
+            field(4),
             field(4),
             field(ITERS - 1, 4, h),
             field(ITERS, 4, h),
@@ -657,8 +754,8 @@
             pltpu.VMEM((ITERS, n, 1, LANES), f32),
             pltpu.SemaphoreType.DMA((4, 3)),
             pltpu.SemaphoreType.DMA((4, 3)),
-            pltpu.SemaphoreType.DMA((4, ITERS, 2)),
-            pltpu.SemaphoreType.DMA((4, ITERS, 2)),
+            pltpu.SemaphoreType.DMA((7, ITERS, 2)),
+            pltpu.SemaphoreType.DMA((7, ITERS, 2)),
             pltpu.SemaphoreType.DMA((ITERS,)),
             pltpu.SemaphoreType.DMA((ITERS,)),
             pltpu.SemaphoreType.DMA((11,)),

time: 43 us -> 40.5 us (0.942)
  Pallas kernels: 42.2 us -> 39.8 us
    pallas_call x1, Pallas kernels: 40.5 us -> 38 us  [per_device(): pl.pallas_call(functools.partial(kernel, slabs, subs, cx, cy, nz), out_sh...]
where the time goes in v3:
time: 40.5 us; the launch traced here: 40.4 us
  Pallas kernels  39.8 us (98%)
  between operations  0.64 us (2%)
    pallas_call x1, Pallas kernels, per_device(): pl.pallas_call(functools.partial(kernel, slabs, subs, cx, cy, nz), out_sh...  38 us
    pallas_call x1, Pallas kernels, per_device(): pl.pallas_call(write, out_shape=(jax.ShapeDtypeStruct((ITERS + 1, 4, cx,...  1.71 us

profile of v3, /device:TPU:0, one launch (start us, length us, event | category | flops | bytes accessed | tf_op | source)
XLA Modules:
  0.0 40.4 jit_solution(4788251660984868600)
XLA Ops:
  0.6 38.0 %shard_map.67 = (f32[4,4,6,16,256]{4,3,2,1,0:T(8,128)S(1)}, f32[3,4,6,16,256]{4,3,2,1,0:T(8,128)S(1)}, f32[16,128]{1,0:T(8,128)S(1)}) custom-call(f32[4,6,16,256]{3,2,1,0:T(8,128)} %start.1, f32[3,6,16,256]{3,2,1,0:T(8,128)} %wind.1, f32[6,16,256]{2,1,0:T(8,128)} %reaction.1, f32[6,16,256]{2,1,0:T(8,128)} %mass.1), custom_call_target="tpu_custom_call" | custom-call | tf_op jit(solution)/shard_map/pallas_call | solution.py:729
  38.7 1.7 %shard_map.68 = (f32[4,4,6,16,256]{4,3,2,1,0:T(8,128)}, f32[3,4,6,16,256]{4,3,2,1,0:T(8,128)}, f32[4,3]{1,0:T(4,128)}) custom-call(f32[4,4,6,16,256]{4,3,2,1,0:T(8,128)S(1)} %get-tuple-element.6.ob, f32[3,4,6,16,256]{4,3,2,1,0:T(8,128)S(1)} %get-tuple-element.7.os_, f32[16,128]{1,0:T(8,128)S(1)} %get-tuple-element.8.scal), custom_call_target="tpu_custom_call" | custom-call | tf_op jit(solution)/shard_map/pallas_call | solution.py:771

commit v4 on v3

--- a/solution.py
+++ b/solution.py
@@ -8,7 +8,7 @@
 from jax.sharding import PartitionSpec as P
 
 ITERS = 3
-UNROLL = 5
+UNROLL = 6
 LANES = 128
 MESH = pl.DeviceIdType.MESH
 
@@ -415,20 +415,22 @@
         yq[e, 0] = (xu[e, 0, h] + 0.5 * qs[e, h]) * co[7, h]
         yq[e, 1] = (xu[e, 0, 1] - 0.5 * qs[e, 3]) * co[7, 1]
 
-    def velocity_edges(e):
-        for k, near, sign in ((-1, 2, -0.5), (h, h + 1, 0.5)):
-            yp, ym, zp, zm = masked(qs[e, k + 2])
-            scale = co[7, k + 1]
-            y0[e, 0, k + 2] = y0[e, 0, k + 2] + (sign * qs[e, near]) * scale
-            y0[e, 1, k + 2] = (xu[e, 1, k + 1] - 0.5 * (yp - ym)) * scale
-            y0[e, 2, k + 2] = (xu[e, 2, k + 1] - 0.5 * (zp - zm)) * scale
-
-    def second_rest(e):
+    def near_across(e):
+        for k in (-1, h):
+            velocity_across(e)(k, 0)
         for c in (1, 2):
             z1[c, 1] = z1[c, 1] + co[1, 1] * y0[e, c, 1] * co[7, 1]
             z1[c, h] = z1[c, h] + co[0, h] * y0[e, c, h + 2] * co[7, h]
         for k in range(h):
-            second(e, 0, k)
+            second(e, 0, k, 1 if k == 0 else 0 if k == h - 1 else None)
+        t1[1] = t1[1] + 0.5 * qs[e, 1] - across(e, 0)
+        t1[h] = t1[h] + 0.5 * qs[e, h + 2] - across(e, h - 1)
+
+    def near_along(e):
+        for k, near, sign in ((-1, 2, -0.5), (h, h + 1, 0.5)):
+            y0[e, 0, k + 2] = y0[e, 0, k + 2] + (sign * qs[e, near]) * co[7, k + 1]
+        z1[0, 1] = z1[0, 1] + co[1, 1] * y0[e, 0, 1] * co[7, 1]
+        z1[0, h] = z1[0, h] + co[0, h] * y0[e, 0, h + 2] * co[7, h]
         second_edges(e, 0)
 
     def second_edges(e, c):
@@ -449,12 +451,6 @@
         full = [y0[e, 0, k + 2] + z1[0, k + 1] for k in range(-1, h + 1)]
         for k in range(h):
             low = t1[k + 1] - 0.5 * (full[k + 2] - full[k])
-            if k == 0:
-                low = low + 0.5 * qs[e, 1]
-            if k == h - 1:
-                low = low + 0.5 * qs[e, h + 2]
-            if k == 0 or k == h - 1:
-                low = low - across(e, k)
             value = mix(low, [xp[i + 1, k + 2] for i in range(e)])
             if e + 1 < ITERS:
                 xp[e + 1, k + 2] = value
@@ -573,9 +569,9 @@
         arrive(2, e)
         velocity_along(e, 0)
         velocity_along(e, h - 1)
+        near_across(e)
         arrive(4, e)
-        velocity_edges(e)
-        second_rest(e)
+        near_along(e)
         image_low(e, factor, weights)
         if e + 1 < ITERS:
             begin(6, e + 1)
@@ -612,6 +608,9 @@
         if e + 1 == ITERS:
             hand_over(2 * ITERS - 1)
 
+        if e + 1 < ITERS:
+            begin(1, e + 1)
+
         def totals(k, acc, e=e):
             acc = list(acc)
             found = [image_of(e, c, k) for c in range(4)]
@@ -630,7 +629,6 @@
         count = e + 2 if e + 1 < ITERS else e + 3
         reduce_start(e, loop(h, totals, (zero,) * count))
         if e + 1 < ITERS:
-            begin(1, e + 1)
             guess_own(e + 1)
 
     for g in range(len(first)):

time: 40.5 us -> 39.9 us (0.985)
  Pallas kernels: 39.8 us -> 39.1 us
    pallas_call x1, Pallas kernels: 38 us -> 37.4 us  [per_device(): pl.pallas_call(functools.partial(kernel, slabs, subs, cx, cy, nz), out_sh...]
where the time goes in v4:
time: 39.9 us; the launch traced here: 39.7 us
  Pallas kernels  39.1 us (98%)
  between operations  0.64 us (2%)
    pallas_call x1, Pallas kernels, per_device(): pl.pallas_call(functools.partial(kernel, slabs, subs, cx, cy, nz), out_sh...  37.4 us
    pallas_call x1, Pallas kernels, per_device(): pl.pallas_call(write, out_shape=(jax.ShapeDtypeStruct((ITERS + 1, 4, cx,...  1.68 us

profile of v4, /device:TPU:0, one launch (start us, length us, event | category | flops | bytes accessed | tf_op | source)
XLA Modules:
  0.0 39.7 jit_solution(6723272081917506266)
XLA Ops:
  0.6 37.4 %shard_map.67 = (f32[4,4,6,16,256]{4,3,2,1,0:T(8,128)S(1)}, f32[3,4,6,16,256]{4,3,2,1,0:T(8,128)S(1)}, f32[16,128]{1,0:T(8,128)S(1)}) custom-call(f32[4,6,16,256]{3,2,1,0:T(8,128)} %start.1, f32[3,6,16,256]{3,2,1,0:T(8,128)} %wind.1, f32[6,16,256]{2,1,0:T(8,128)} %reaction.1, f32[6,16,256]{2,1,0:T(8,128)} %mass.1), custom_call_target="tpu_custom_call" | custom-call | tf_op jit(solution)/shard_map/pallas_call | solution.py:727
  38.1 1.7 %shard_map.68 = (f32[4,4,6,16,256]{4,3,2,1,0:T(8,128)}, f32[3,4,6,16,256]{4,3,2,1,0:T(8,128)}, f32[4,3]{1,0:T(4,128)}) custom-call(f32[4,4,6,16,256]{4,3,2,1,0:T(8,128)S(1)} %get-tuple-element.6.ob, f32[3,4,6,16,256]{4,3,2,1,0:T(8,128)S(1)} %get-tuple-element.7.os_, f32[16,128]{1,0:T(8,128)S(1)} %get-tuple-element.8.scal), custom_call_target="tpu_custom_call" | custom-call | tf_op jit(solution)/shard_map/pallas_call | solution.py:769

commit v5 on v4

--- a/solution.py
+++ b/solution.py
@@ -89,7 +89,6 @@
         item.start()
     for item in own:
         item.start()
-    first_out.start()
 
     barrier = pltpu.get_barrier_semaphore()
 
@@ -505,6 +504,7 @@
     loop(h, masses, low=1)
     further(1)
     own[0].wait()
+    first_out.start()
     first_near(0)
     guess_own(0)
     first_far(0)
@@ -564,7 +564,6 @@
                 return carry
 
             loop(h, form)
-            hand_over(ITERS + e - 1)
             arrive(1, e)
         arrive(2, e)
         velocity_along(e, 0)
@@ -593,7 +592,6 @@
         second_edges(e, 1)
         second_edges(e, 2)
         loop(h, image(e, factor, weights))
-        hand_over(e)
         if e == 0:
             further(len(steps))
         arrive(5, e)
@@ -605,9 +603,6 @@
             else:
                 wl[c, 0] = wl[c, 0] - ca[2] * below
                 wl[c, h - 1] = wl[c, h - 1] - ca[3] * above
-        if e + 1 == ITERS:
-            hand_over(2 * ITERS - 1)
-
         if e + 1 < ITERS:
             begin(1, e + 1)
 
@@ -631,6 +626,8 @@
         if e + 1 < ITERS:
             guess_own(e + 1)
 
+    for i in range(2 * ITERS):
+        hand_over(i)
     for g in range(len(first)):
         first_finish(g)
     first_out.wait()

time: 39.9 us -> 39.9 us (level)
  no operation moved by 1% of the time
where the time goes in v5:
time: 39.9 us; the launch traced here: 39.7 us
  Pallas kernels  39.1 us (98%)
  between operations  0.64 us (2%)
    pallas_call x1, Pallas kernels, per_device(): pl.pallas_call(functools.partial(kernel, slabs, subs, cx, cy, nz), out_sh...  37.4 us
    pallas_call x1, Pallas kernels, per_device(): pl.pallas_call(write, out_shape=(jax.ShapeDtypeStruct((ITERS + 1, 4, cx,...  1.68 us

profile of v5, /device:TPU:0, one launch (start us, length us, event | category | flops | bytes accessed | tf_op | source)
XLA Modules:
  0.0 39.7 jit_solution(11925207852825505942)
XLA Ops:
  0.6 37.4 %shard_map.67 = (f32[4,4,6,16,256]{4,3,2,1,0:T(8,128)S(1)}, f32[3,4,6,16,256]{4,3,2,1,0:T(8,128)S(1)}, f32[16,128]{1,0:T(8,128)S(1)}) custom-call(f32[4,6,16,256]{3,2,1,0:T(8,128)} %start.1, f32[3,6,16,256]{3,2,1,0:T(8,128)} %wind.1, f32[6,16,256]{2,1,0:T(8,128)} %reaction.1, f32[6,16,256]{2,1,0:T(8,128)} %mass.1), custom_call_target="tpu_custom_call" | custom-call | tf_op jit(solution)/shard_map/pallas_call | solution.py:724
  38.0 1.7 %shard_map.68 = (f32[4,4,6,16,256]{4,3,2,1,0:T(8,128)}, f32[3,4,6,16,256]{4,3,2,1,0:T(8,128)}, f32[4,3]{1,0:T(4,128)}) custom-call(f32[4,4,6,16,256]{4,3,2,1,0:T(8,128)S(1)} %get-tuple-element.6.ob, f32[3,4,6,16,256]{4,3,2,1,0:T(8,128)S(1)} %get-tuple-element.7.os_, f32[16,128]{1,0:T(8,128)S(1)} %get-tuple-element.8.scal), custom_call_target="tpu_custom_call" | custom-call | tf_op jit(solution)/shard_map/pallas_call | solution.py:766
